TPU v7x, 256 devices: a whole 4x4x8 slice. The times are simulated.
256 devices in a mesh: dp: 64 (over z, y, core), tp: 4 (over x).
Axes of the slice: x: 4, y: 4, z: 8, core: 2. Of those that a mesh axis runs over, the one named last changes fastest.
Arguments:
- partial_up: bfloat16 [64, 1024, 4096], P('dp', None, 'tp'), may hold values from -8 to 8
- partial_down: bfloat16 [64, 4096, 1024], P('dp', 'tp'), may hold values from -8 to 8
- partial_norm: bfloat16 [64, 1024], P('dp'), may hold values from -16 to 16
- master_up: float32 [1024, 4096], P('dp', 'tp'), may hold values from -0.5 to 0.5
- master_down: float32 [4096, 1024], P('tp', 'dp'), may hold values from -0.25 to 0.25
- master_norm: float32 [1024], P('dp'), may hold values from 0.25 to 1.75
- memory_up: float32 [1024, 4096], P('dp', 'tp'), may hold values from 0.0001953125 to 0.001953125
- memory_down: float32 [4096, 1024], P('tp', 'dp'), may hold values from 4.8828126e-05 to 0.00048828125
- memory_norm: float32 [1024], P('dp'), may hold values from 0.05 to 0.8
Outputs:
- compute_up: bfloat16 [1024, 4096], P(None, 'tp')
- compute_down: bfloat16 [4096, 1024], P('tp')
- compute_norm: bfloat16 [1024], replicated
- stepped_up: float32 [1024, 4096], P('dp', 'tp')
- stepped_down: float32 [4096, 1024], P('tp', 'dp')
- stepped_norm: float32 [1024], P('dp')
- state_new_up: float32 [1024, 4096], P('dp', 'tp')
- state_new_down: float32 [4096, 1024], P('tp', 'dp')
- state_new_norm: float32 [1024], P('dp')
All inputs are finite; a program needn't handle non-finite values.
Results may differ from a plain program's by a relative error of at most 0.001.
Values may be sent and summed in bfloat16 or wider, within the bound.
A program may use at most 64 MiB of HBM per device.

v0:
```python
import jax
import jax.numpy as jnp
from jax import lax
from jax.sharding import Mesh
from jax.sharding import PartitionSpec as P

DP = ("dp_0", "dp_1", "dp_2")
learn_rate = 0.025
hold_rate = 0.8


def cut_along(array, dim, size):
    before, after = (array.shape[:dim], array.shape[dim + 1 :])
    return jnp.moveaxis(array.reshape(*before, size, -1, *after), dim, 0)


def sum_packed(arrays, axis, dims):
    size = lax.axis_size(axis)
    pieces = [cut_along(a, dim, size) for a, dim in zip(arrays, dims)]
    lines = jnp.concatenate([b.reshape(size, -1) for b in pieces], axis=1)
    width = max(16, -(-lines.shape[1] // 1024) * 8)
    lines = jnp.pad(lines, ((0, 0), (0, width * 128 - lines.shape[1]))).reshape(-1, 128)
    vector, at, gathered = (lax.psum_scatter(lines, axis, tiled=True).reshape(-1), 0, [])
    for b in pieces:
        part = b[0]
        gathered.append(vector[at : at + part.size].reshape(part.shape))
        at += part.size
    return tuple(gathered)


def over_axes(array, axes):
    for axis in axes:
        array = lax.psum(array, axis)
    return array


def sent_to_all(array, axis):
    copies = jnp.broadcast_to(array, (lax.axis_size(axis), *array.shape))
    return lax.all_to_all(copies, axis, split_axis=0, concat_axis=0, tiled=True)


def of_everyone(array, axis):
    everything = sent_to_all(array, axis)
    return jnp.sum(everything, axis=0)


def in_one(arrays, axis):
    ends = [0]
    for a in arrays:
        ends.append(ends[-1] + a.size)
    running = of_everyone(jnp.concatenate([a.ravel() for a in arrays]), axis)
    return tuple((running[b:e].reshape(a.shape) for a, b, e in zip(arrays, ends, ends[1:])))


def turned_gather(arrays, axis, dims):
    turned = [jnp.moveaxis(a, dim, 0) for a, dim in zip(arrays, dims)]
    widths = [t[0].size for t in turned]
    both = jnp.concatenate([t.reshape(-1, w) for t, w in zip(turned, widths)], axis=1)
    filled = lax.all_gather(both, axis, axis=0, tiled=True)
    pieces = jnp.split(filled, [sum(widths[:k]) for k in range(1, len(widths))], axis=1)
    return tuple(
        (
            jnp.moveaxis(b.reshape(-1, *t.shape[1:]), 0, dim)
            for b, t, dim in zip(pieces, turned, dims)
        )
    )


def local(
    partial_up,
    partial_down,
    partial_norm,
    master_up,
    master_down,
    master_norm,
    memory_up,
    memory_down,
    memory_norm,
):
    mean_up, mean_down = sum_packed(
        (partial_up[0].astype(jnp.float32), partial_down[0].astype(jnp.float32)), DP, (0, 1)
    )
    whole_norm = over_axes(partial_norm[0].astype(jnp.float32), DP)
    place = lax.axis_index(DP)
    mean_norm = lax.dynamic_slice_in_dim(
        whole_norm, place * master_norm.shape[0], master_norm.shape[0]
    )
    mean_rate = lax.axis_size(DP) ** (-0.5)
    mean_up = mean_up * mean_rate
    mean_down = mean_down * mean_rate
    mean_norm = mean_norm * mean_rate
    own_up, own_down, slope_up_norm, slope_down_norm = in_one(
        (
            jnp.sum(master_up * master_up, axis=1, keepdims=True),
            jnp.sum(master_down * master_down, axis=0, keepdims=True),
            jnp.sum(mean_up * mean_up, axis=1, keepdims=True),
            jnp.sum(mean_down * mean_down, axis=0, keepdims=True),
        ),
        "tp",
    )
    mean_up = mean_up * (jnp.sqrt(own_up) * lax.rsqrt(slope_up_norm + 1e-06))
    mean_down = mean_down * (jnp.sqrt(own_down) * lax.rsqrt(slope_down_norm + 1e-06))
    state_new_up = hold_rate * memory_up + (1.0 - hold_rate) * mean_up * mean_up
    stepped_up = master_up - learn_rate * mean_up * lax.rsqrt(state_new_up + 1e-06)
    state_new_down = hold_rate * memory_down + (1.0 - hold_rate) * mean_down * mean_down
    stepped_down = master_down - learn_rate * mean_down * lax.rsqrt(state_new_down + 1e-06)
    state_new_norm = hold_rate * memory_norm + (1.0 - hold_rate) * mean_norm * mean_norm
    stepped_norm = master_norm - learn_rate * mean_norm * lax.rsqrt(state_new_norm + 1e-06)
    compute_up, compute_down, compute_norm = turned_gather(
        (
            stepped_up.astype(jnp.bfloat16),
            stepped_down.astype(jnp.bfloat16),
            stepped_norm.astype(jnp.bfloat16),
        ),
        DP,
        (0, 1, 0),
    )
    return (
        compute_up,
        compute_down,
        compute_norm,
        stepped_up,
        stepped_down,
        stepped_norm,
        state_new_up,
        state_new_down,
        state_new_norm,
    )


def solution(mesh):
    finer = Mesh(mesh.devices.reshape(8, 4, 2, mesh.shape["tp"]), ("dp_0", "dp_1", "dp_2", "tp"))
    return jax.shard_map(
        local,
        mesh=finer,
        in_specs=(
            P(DP, None, "tp"),
            P(DP, "tp", None),
            P(DP, None),
            P(DP, "tp"),
            P("tp", DP),
            P(DP),
            P(DP, "tp"),
            P("tp", DP),
            P(DP),
        ),
        out_specs=(
            P(None, "tp"),
            P("tp", None),
            P(),
            P(DP, "tp"),
            P("tp", DP),
            P(DP),
            P(DP, "tp"),
            P("tp", DP),
            P(DP),
        ),
        check_vma=False,
    )
```

profile of v0, /device:TPU:1, one launch (start us, length us, event | category | flops | bytes accessed | tf_op | source)
XLA Modules:
  0.0 300.1 jit_solution(11367496237568048185)
XLA Ops:
  7.2 0.0 reduce-scatter.2.cloned.1.call-start
  7.2 2.9 copy.45
  10.1 6.1 %copy.46 = bf16[64,1024,16]{0,2,1:T(8,128)(2,1)} copy(bf16[64,1024,16]{1,2,0:T(8,128)(2,1)S(1)} %bitcast.13) | data formatting | bytes 4194304 | tf_op jit(solution)/shard_map/transpose | solution.py:14
  16.2 3.5 %copy.47 = bf16[64,16384]{1,0:T(8,128)(2,1)S(1)} copy(bf16[64,16384]{0,1:T(8,128)(2,1)} %bitcast.12) | data formatting | bytes 4194304 | tf_op jit(solution)/shard_map/reshape | solution.py:20
  19.8 4.2 %convert_element_type.25 = bf16[64,16384]{1,0:T(8,128)(2,1)} reshape(bf16[1,1024,1024]{2,1,0:T(8,128)(2,1)} %param.9) | data formatting | bytes 4194304 | tf_op jit(solution)/shard_map/convert_element_type | solution.py:81
  23.9 5.3 %maximum_convert_fusion = f32[64,32768]{1,0:T(8,128)} fusion(bf16[64,16384]{1,0:T(8,128)(2,1)S(1)} %copy.47, bf16[64,16384]{1,0:T(8,128)(2,1)} %convert_element_type.25), kind=kLoop, calls=%fused_computation | loop fusion | flops 8388608 | bytes 12582912 | tf_op jit(solution)/shard_map/reshape | solution.py:22
  29.3 9.3 %reshape.81 = f32[16384,128]{1,0:T(8,128)} reshape(f32[64,32768]{1,0:T(8,128)} %maximum_convert_fusion) | data formatting | bytes 16777216 | tf_op jit(solution)/shard_map/reshape | solution.py:22
  38.6 0.0 copy-start.4
  38.6 0.0 copy-start
  38.6 0.0 copy-start.1
  38.6 0.0 copy-start.5
  38.6 0.0 copy-start.6
  38.6 0.0 copy-start.2
  38.6 0.0 copy-start.3
  38.6 0.0 reduce-scatter.2.cloned.1.call-update
  38.7 0.6 copy-done.4
  39.3 17.3 %psum.21 = f32[1024]{0:T(1024)S(1)} all-reduce(f32[1024]{0:T(1024)S(1)} %bitcast.14), channel_id=1, replica_groups=mesh['dp_0'=8,'dp_1'=4,'dp_2'=2,'tp'=4] {'dp_0'}, use_global_device_ids=true, to_apply=%region_7.8 | all-reduce | flops 1024 | bytes 8192 | tf_op jit(solution)/shard_map/psum | solution.py:33
  56.6 8.7 %psum.22 = f32[1024]{0:T(1024)S(1)} all-reduce(f32[1024]{0:T(1024)S(1)} %psum.21), channel_id=1, replica_groups=mesh['dp_0'=8,'dp_1'=4,'dp_2'=2,'tp'=4] {'dp_1'}, use_global_device_ids=true, to_apply=%region_8.9 | all-reduce | flops 1024 | bytes 8192 | tf_op jit(solution)/shard_map/psum | solution.py:33
  65.3 8.3 %psum.23 = f32[1024]{0:T(1024)S(1)} all-reduce(f32[1024]{0:T(1024)S(1)} %psum.22), channel_id=1, replica_groups=mesh['dp_0'=8,'dp_1'=4,'dp_2'=2,'tp'=4] {'dp_2'}, use_global_device_ids=true, to_apply=%region_9.10 | all-reduce | flops 1024 | bytes 8192 | tf_op jit(solution)/shard_map/psum | solution.py:33
  73.6 0.0 copy-done
  73.6 0.1 multiply_reduce_fusion.2
  73.7 0.0 copy-done.1
  73.8 0.1 multiply_reduce_fusion.3
  73.9 116.3 %reduce-scatter.2.cloned.1.call-done = f32[256,128]{1,0:T(8,128)} async-done(((f32[16384,128]{1,0:T(8,128)}), f32[256,128]{1,0:T(8,128)}) %reduce-scatter.2.cloned.1.call-update) | async-done | bytes 131088 | tf_op jit(solution)/shard_map/reduce_scatter | solution.py:23
  190.1 1.0 fusion.5
  191.1 0.2 reshape.77
  191.3 0.2 multiply_reduce_fusion
  191.5 0.1 reduce_sum.55
  191.5 0.1 reduce_sum.56
  191.7 0.1 pad_maximum_fusion.1
  191.7 0.6 broadcast_in_dim.3
  192.3 4.4 %all-to-all-start = ((f32[4,1,64]{2,1,0:T(1,128)}), f32[4,1,64]{2,1,0:T(1,128)S(1)}, u32[]{:S(2)}, u32[]{:S(2)}) async-start(f32[4,1,64]{2,1,0:T(1,128)} %broadcast_in_dim.3), calls=%async_computation.1 | async-start | bytes 4096 | tf_op jit(solution)/shard_map/all_to_all | solution.py:39
  196.7 0.0 all-gather.2.cloned.1.call-start
  196.7 0.0 copy-done.5
  196.7 0.0 copy-done.6
  196.7 0.6 convert_bitcast_fusion.1
  197.3 0.1 copy.50
  197.4 0.2 copy.49
  197.6 3.2 %all-to-all-done = f32[4,1,64]{2,1,0:T(1,128)S(1)} async-done(((f32[4,1,64]{2,1,0:T(1,128)}), f32[4,1,64]{2,1,0:T(1,128)S(1)}, u32[]{:S(2)}, u32[]{:S(2)}) %all-to-all-start) | async-done | bytes 1056 | tf_op jit(solution)/shard_map/all_to_all | solution.py:39
  200.8 0.1 multiply_multiply_fusion.3
  200.9 0.0 copy-done.2
  200.9 0.7 convert_bitcast_fusion
  201.6 0.0 copy-done.3
  201.6 0.7 fusion.2
  202.4 0.6 pad_maximum_fusion
  203.0 0.0 all-gather.2.cloned.1.call-update
  203.0 82.0 %all-gather.2.cloned.1.call-done = bf16[1024,2049]{1,0:T(8,128)(2,1)} async-done(((bf16[16,2049]{1,0:T(8,128)(2,1)}), bf16[1024,2049]{1,0:T(8,128)(2,1)}) %all-gather.2.cloned.1.call-update) | async-done | bytes 4196368 | tf_op jit(solution)/shard_map/all_gather | solution.py:59
  285.0 4.0 %slice_bitcast_fusion = (bf16[1024,1024]{0,1:T(8,128)(2,1)S(1)}, bf16[1024,1024]{1,0:T(8,128)(2,1)}) fusion(bf16[1024,2049]{1,0:T(8,128)(2,1)} %all-gather.2.cloned.1.call-done), kind=kLoop, calls=%fused_computation.1 | loop fusion | bytes 8388608 | tf_op jit(solution)/shard_map/transpose | solution.py:63
  289.0 2.5 copy.51
  291.6 1.7 slice_reduce_fusion
  (3 shorter events, 0.0 us)
Async XLA Ops:
  7.2 183.0 %reduce-scatter.2.cloned.1.call-start = ((), (), s32[]{:S(2)}) async-start(), calls=%async_computation.2 | async-start | bytes 8519680 | tf_op jit(solution)/shard_map/reduce_scatter | solution.py:23
  38.6 0.7 copy-start.4
  38.6 35.0 %copy-start = (f32[1024,16]{0,1:T(8,128)S(1)}, f32[1024,16]{0,1:T(8,128)}, u32[]{:S(2)}) copy-start(f32[1024,16]{0,1:T(8,128)} %param.13) | copy-start | bytes 196612
  38.6 35.2 %copy-start.1 = (f32[16,1024]{1,0:T(8,128)S(1)}, f32[16,1024]{1,0:T(8,128)}, u32[]{:S(2)}) copy-start(f32[16,1024]{1,0:T(8,128)} %param.12) | copy-start | bytes 196612
  38.6 158.1 %copy-start.5 = (f32[16]{0:T(128)S(1)}, f32[16]{0:T(128)}, u32[]{:S(2)}) copy-start(f32[16]{0:T(128)} %param.14) | copy-start | bytes 196
  38.6 158.1 %copy-start.6 = (f32[16]{0:T(128)S(1)}, f32[16]{0:T(128)}, u32[]{:S(2)}) copy-start(f32[16]{0:T(128)} %param.17) | copy-start | bytes 196
  38.6 162.3 %copy-start.2 = (f32[1024,16]{0,1:T(8,128)S(1)}, f32[1024,16]{0,1:T(8,128)}, u32[]{:S(2)}) copy-start(f32[1024,16]{0,1:T(8,128)} %param.16) | copy-start | bytes 196612
  38.6 163.0 %copy-start.3 = (f32[16,1024]{1,0:T(8,128)S(1)}, f32[16,1024]{1,0:T(8,128)}, u32[]{:S(2)}) copy-start(f32[16,1024]{1,0:T(8,128)} %param.15) | copy-start | bytes 196612
  192.3 8.4 %all-to-all-start = ((f32[4,1,64]{2,1,0:T(1,128)}), f32[4,1,64]{2,1,0:T(1,128)S(1)}, u32[]{:S(2)}, u32[]{:S(2)}) async-start(f32[4,1,64]{2,1,0:T(1,128)} %broadcast_in_dim.3), calls=%async_computation.1 | async-start | bytes 4096 | tf_op jit(solution)/shard_map/all_to_all | solution.py:39
  196.7 88.3 %all-gather.2.cloned.1.call-start = ((), (), s32[]{:S(2)}) async-start(), calls=%async_computation.3 | async-start | bytes 4526080 | tf_op jit(solution)/shard_map/all_gather | solution.py:59
Sparse Core Ops, SparseCore 0:
  38.8 151.3 reduce-scatter.1
  203.1 81.8 all-gather.1
where the time goes:
time: 301 us; the launch traced here: 300 us
  waiting for transfers between devices  201 us (67%)
  local copies, waits for them, and re-layouts  36 us (12%)
  blocking collectives  34.4 us (11%)
  between operations  14.1 us (5%)
  other arithmetic  9.73 us (3%)
  starting transfers between devices  4.42 us (1%)
    reduce_scatter x1, waiting for transfers between devices, sum_packed(): lax.psum_scatter(lines, axis, tiled=True).reshape(-1)  116 us
    all_gather x1, waiting for transfers between devices, turned_gather(): filled = lax.all_gather(both, axis, axis=0, tiled=True)  82 us
    psum x3, blocking collectives, over_axes(): array = lax.psum(array, axis)  34.4 us
    reshape x1, local copies, waits for them, and re-layouts, sum_packed(): jnp.pad(lines, ((0, 0), (0, width * 128 - lines.shape[1]))).reshape(-1, 128)  9.28 us
    transpose x1, local copies, waits for them, and re-layouts, cut_along(): return jnp.moveaxis(array.reshape(*before, size, -1, *after), dim, 0)  6.13 us
    unnamed x16, local copies, waits for them, and re-layouts  6.03 us
  transfers between devices with their start and end apart: 3, of which 3 were waited for; matrix products, arithmetic and copies ran while one was open for 0% of the time, Pallas kernels for 0%

commit v1 on v0

--- a/solution.py
+++ b/solution.py
@@ -7,6 +7,13 @@
 DP = ("dp_0", "dp_1", "dp_2")
 learn_rate = 0.025
 hold_rate = 0.8
+
+
+def exchange_gather(x, axis, along):
+    size = lax.axis_size(axis)
+    blocks = jnp.stack([x for _ in range(size)])
+    blocks = lax.all_to_all(blocks, axis, split_axis=0, concat_axis=0)
+    return jnp.concatenate(blocks, axis=along)
 
 
 def cut_along(array, dim, size):
@@ -56,7 +63,7 @@
     turned = [jnp.moveaxis(a, dim, 0) for a, dim in zip(arrays, dims)]
     widths = [t[0].size for t in turned]
     both = jnp.concatenate([t.reshape(-1, w) for t, w in zip(turned, widths)], axis=1)
-    filled = lax.all_gather(both, axis, axis=0, tiled=True)
+    filled = exchange_gather(both, axis, 0)
     pieces = jnp.split(filled, [sum(widths[:k]) for k in range(1, len(widths))], axis=1)
     return tuple(
         (

time: 301 us -> 332 us (1.10)
  blocking collectives: 34.4 us -> 151 us
  waiting for transfers between devices: 201 us -> 119 us
    all_to_all x0 -> x1, blocking collectives: none -> 116 us  [exchange_gather(): blocks = lax.all_to_all(blocks, axis, split_axis=0, concat_axis=0)]
    all_gather x1 -> x0, waiting for transfers between devices: 82 us -> none  [turned_gather(): filled = lax.all_gather(both, axis, axis=0, tiled=True)]
  transfers between devices with their start and end apart: 3 -> 2, of which waited for: 3 -> 2; matrix products, arithmetic and copies ran while one was open for 0% -> 0% of each run, Pallas kernels for 0% -> 0%
where the time goes in v1:
time: 332 us; the launch traced here: 331 us
  blocking collectives  151 us (45%)
  waiting for transfers between devices  119 us (36%)
  local copies, waits for them, and re-layouts  33.3 us (10%)
  between operations  14.1 us (4%)
  other arithmetic  9.1 us (3%)
  starting transfers between devices  4.42 us (1%)
    all_to_all x1, blocking collectives, exchange_gather(): blocks = lax.all_to_all(blocks, axis, split_axis=0, concat_axis=0)  116 us
    reduce_scatter x1, waiting for transfers between devices, sum_packed(): lax.psum_scatter(lines, axis, tiled=True).reshape(-1)  116 us
    psum x3, blocking collectives, over_axes(): array = lax.psum(array, axis)  34.4 us
    reshape x1, local copies, waits for them, and re-layouts, sum_packed(): jnp.pad(lines, ((0, 0), (0, width * 128 - lines.shape[1]))).reshape(-1, 128)  9.28 us
  transfers between devices with their start and end apart: 2, of which 2 were waited for; matrix products, arithmetic and copies ran while one was open for 0% of the time, Pallas kernels for 0%

profile of v1, /device:TPU:1, one launch (start us, length us, event | category | flops | bytes accessed | tf_op | source)
XLA Modules:
  0.0 331.1 jit_solution(3168704832149935460)
XLA Ops:
  7.2 0.0 reduce-scatter.2.cloned.1.call-start
  7.2 2.9 copy.47
  10.1 6.1 %copy.48 = bf16[64,1024,16]{0,2,1:T(8,128)(2,1)} copy(bf16[64,1024,16]{1,2,0:T(8,128)(2,1)S(1)} %bitcast.16) | data formatting | bytes 4194304 | tf_op jit(solution)/shard_map/transpose | solution.py:21
  16.2 3.5 %copy.49 = bf16[64,16384]{1,0:T(8,128)(2,1)S(1)} copy(bf16[64,16384]{0,1:T(8,128)(2,1)} %bitcast.15) | data formatting | bytes 4194304 | tf_op jit(solution)/shard_map/reshape | solution.py:27
  19.8 4.2 %convert_element_type.25 = bf16[64,16384]{1,0:T(8,128)(2,1)} reshape(bf16[1,1024,1024]{2,1,0:T(8,128)(2,1)} %param.9) | data formatting | bytes 4194304 | tf_op jit(solution)/shard_map/convert_element_type | solution.py:88
  23.9 5.3 %maximum_convert_fusion = f32[64,32768]{1,0:T(8,128)} fusion(bf16[64,16384]{1,0:T(8,128)(2,1)S(1)} %copy.49, bf16[64,16384]{1,0:T(8,128)(2,1)} %convert_element_type.25), kind=kLoop, calls=%fused_computation | loop fusion | flops 8388608 | bytes 12582912 | tf_op jit(solution)/shard_map/reshape | solution.py:29
  29.3 9.3 %reshape.87 = f32[16384,128]{1,0:T(8,128)} reshape(f32[64,32768]{1,0:T(8,128)} %maximum_convert_fusion) | data formatting | bytes 16777216 | tf_op jit(solution)/shard_map/reshape | solution.py:29
  38.6 0.0 copy-start.4
  38.6 0.0 copy-start
  38.6 0.0 copy-start.1
  38.6 0.0 copy-start.5
  38.6 0.0 copy-start.6
  38.6 0.0 copy-start.2
  38.6 0.0 copy-start.3
  38.6 0.0 reduce-scatter.2.cloned.1.call-update
  38.7 0.6 copy-done.4
  39.3 17.3 %psum.21 = f32[1024]{0:T(1024)S(1)} all-reduce(f32[1024]{0:T(1024)S(1)} %bitcast.17), channel_id=1, replica_groups=mesh['dp_0'=8,'dp_1'=4,'dp_2'=2,'tp'=4] {'dp_0'}, use_global_device_ids=true, to_apply=%region_7.8 | all-reduce | flops 1024 | bytes 8192 | tf_op jit(solution)/shard_map/psum | solution.py:40
  56.6 8.7 %psum.22 = f32[1024]{0:T(1024)S(1)} all-reduce(f32[1024]{0:T(1024)S(1)} %psum.21), channel_id=1, replica_groups=mesh['dp_0'=8,'dp_1'=4,'dp_2'=2,'tp'=4] {'dp_1'}, use_global_device_ids=true, to_apply=%region_8.9 | all-reduce | flops 1024 | bytes 8192 | tf_op jit(solution)/shard_map/psum | solution.py:40
  65.3 8.3 %psum.23 = f32[1024]{0:T(1024)S(1)} all-reduce(f32[1024]{0:T(1024)S(1)} %psum.22), channel_id=1, replica_groups=mesh['dp_0'=8,'dp_1'=4,'dp_2'=2,'tp'=4] {'dp_2'}, use_global_device_ids=true, to_apply=%region_9.10 | all-reduce | flops 1024 | bytes 8192 | tf_op jit(solution)/shard_map/psum | solution.py:40
  73.6 0.0 copy-done
  73.6 0.1 multiply_reduce_fusion.2
  73.7 0.0 copy-done.1
  73.8 0.1 multiply_reduce_fusion.3
  73.9 116.3 %reduce-scatter.2.cloned.1.call-done = f32[256,128]{1,0:T(8,128)} async-done(((f32[16384,128]{1,0:T(8,128)}), f32[256,128]{1,0:T(8,128)}) %reduce-scatter.2.cloned.1.call-update) | async-done | bytes 131088 | tf_op jit(solution)/shard_map/reduce_scatter | solution.py:30
  190.1 1.0 fusion.5
  191.1 0.2 reshape.82
  191.3 0.2 multiply_reduce_fusion
  191.5 0.1 reduce_sum.55
  191.5 0.1 reduce_sum.56
  191.7 0.1 pad_maximum_fusion.1
  191.7 0.6 broadcast_in_dim.3
  192.3 4.4 %all-to-all-start = ((f32[4,1,64]{2,1,0:T(1,128)}), f32[4,1,64]{2,1,0:T(1,128)S(1)}, u32[]{:S(2)}, u32[]{:S(2)}) async-start(f32[4,1,64]{2,1,0:T(1,128)} %broadcast_in_dim.3), calls=%async_computation.1 | async-start | bytes 4096 | tf_op jit(solution)/shard_map/all_to_all | solution.py:46
  196.7 0.0 copy-done.5
  196.7 0.0 copy-done.6
  196.7 0.6 convert_bitcast_fusion.1
  197.3 0.1 copy.52
  197.4 0.2 copy.51
  197.6 3.2 all-to-all-done
  200.8 0.1 multiply_multiply_fusion.3
  200.9 0.0 copy-done.2
  200.9 0.7 convert_bitcast_fusion
  201.6 0.0 copy-done.3
  201.6 0.7 fusion.2
  202.4 0.3 stack.2
  202.7 116.4 %all_to_all.11 = bf16[64,16,2049]{2,1,0:T(8,128)(2,1)S(1)} all-to-all(bf16[64,16,2049]{2,1,0:T(8,128)(2,1)S(1)} %stack.2), channel_id=1, replica_groups=mesh['dp_0'=8,'dp_1'=4,'dp_2'=2,'tp'=4] {'dp_0','dp_1','dp_2'}, dimensions={0} | all-to-all | bytes 8392704 | tf_op jit(solution)/shard_map/all_to_all | solution.py:15
  319.1 1.9 slice_bitcast_fusion
  321.0 0.7 slice_reduce_fusion
  321.7 2.5 copy.53
  (4 shorter events, 0.1 us)
Async XLA Ops:
  7.2 183.0 %reduce-scatter.2.cloned.1.call-start = ((), (), s32[]{:S(2)}) async-start(), calls=%async_computation.3 | async-start | bytes 8519680 | tf_op jit(solution)/shard_map/reduce_scatter | solution.py:30
  38.6 0.7 copy-start.4
  38.6 35.0 %copy-start = (f32[1024,16]{0,1:T(8,128)S(1)}, f32[1024,16]{0,1:T(8,128)}, u32[]{:S(2)}) copy-start(f32[1024,16]{0,1:T(8,128)} %param.13) | copy-start | bytes 196612
  38.6 35.2 %copy-start.1 = (f32[16,1024]{1,0:T(8,128)S(1)}, f32[16,1024]{1,0:T(8,128)}, u32[]{:S(2)}) copy-start(f32[16,1024]{1,0:T(8,128)} %param.12) | copy-start | bytes 196612
  38.6 158.1 %copy-start.5 = (f32[16]{0:T(128)S(1)}, f32[16]{0:T(128)}, u32[]{:S(2)}) copy-start(f32[16]{0:T(128)} %param.14) | copy-start | bytes 196
  38.6 158.1 %copy-start.6 = (f32[16]{0:T(128)S(1)}, f32[16]{0:T(128)}, u32[]{:S(2)}) copy-start(f32[16]{0:T(128)} %param.17) | copy-start | bytes 196
  38.6 162.3 %copy-start.2 = (f32[1024,16]{0,1:T(8,128)S(1)}, f32[1024,16]{0,1:T(8,128)}, u32[]{:S(2)}) copy-start(f32[1024,16]{0,1:T(8,128)} %param.16) | copy-start | bytes 196612
  38.6 163.0 %copy-start.3 = (f32[16,1024]{1,0:T(8,128)S(1)}, f32[16,1024]{1,0:T(8,128)}, u32[]{:S(2)}) copy-start(f32[16,1024]{1,0:T(8,128)} %param.15) | copy-start | bytes 196612
  192.3 8.4 %all-to-all-start = ((f32[4,1,64]{2,1,0:T(1,128)}), f32[4,1,64]{2,1,0:T(1,128)S(1)}, u32[]{:S(2)}, u32[]{:S(2)}) async-start(f32[4,1,64]{2,1,0:T(1,128)} %broadcast_in_dim.3), calls=%async_computation.1 | async-start | bytes 4096 | tf_op jit(solution)/shard_map/all_to_all | solution.py:46
Sparse Core Ops, SparseCore 0:
  38.8 151.3 reduce-scatter.1
